TPU v7x, 32 devices: a whole 2x2x4 slice. The times are simulated.
32 devices in a mesh: gx: 8 (over y, x, core), gy: 4 (over z).
Axes of the slice: x: 2, y: 2, z: 4, core: 2. Of those that a mesh axis runs over, the one named last changes fastest.
Arguments:
- sat_new: float32 [64, 512, 512], P(None, 'gx', 'gy'), may hold values from 0.02 to 1
- sat_old: float32 [64, 512, 512], P(None, 'gx', 'gy'), may hold values from 0.1 to 0.95
- porosity: float32 [64, 512, 512], P(None, 'gx', 'gy'), may hold values from 0.1 to 0.5
- spec_storage: float32 [64, 512, 512], P(None, 'gx', 'gy'), may hold values from 0.01 to 0.2
- pressure: float32 [64, 512, 512], P(None, 'gx', 'gy'), may hold values from -6 to 6
- conduct: float32 [64, 512, 512], P(None, 'gx', 'gy'), may hold values from 0.1 to 1
- et_rate: float32 [64, 512, 512], P(None, 'gx', 'gy'), may hold values from 0 to 1
- thickness: float32 [64], replicated, may hold values from 0.005 to 0.05
- labels: int32 [512, 512], P('gx', 'gy'), may hold values from 0 to 511, as said below
- outlet: int32 [512, 512], P('gx', 'gy'), may hold values 0 or 1
Outputs:
- basin_totals: float32 [4, 64, 512], replicated
- column_balance: float32 [4, 512, 512], P(None, 'gx', 'gy')
- peak_change: float32 [], replicated
Inputs may be any that keep to these rules, and one draw needn't show every extreme that they name: `labels`: subbasins are contiguous patches of columns with ragged edges.
All inputs are finite; a program needn't handle non-finite values. No bound on the sum of `outlet` on one device may be relied on, other than what follows from the above.
Results may differ from a plain program's by a relative error of at most 0.00016.
Values sent between devices are 32-bit elements; how exact they have to be, the bound alone decides.
A program may use at most 128 MiB of HBM per device.

v0:
```python
import functools

import jax
import jax.numpy as jnp
from jax import lax
from jax.experimental import pallas as pl
from jax.experimental.pallas import tpu as pltpu
from jax.sharding import PartitionSpec as P

SUB = 512
LANES = 128
STEP = 8
GROUP = 4
ZBLOCK = 32
MESH = pl.DeviceIdType.MESH
VMEM_LIMIT = 60 * 1024 * 1024


def flow(p, k, pn, kn):
    return 2.0 * k * kn / (k + kn) * (p - pn)


def split(value):
    high = value.astype(jnp.bfloat16)
    return high, (value - high.astype(jnp.float32)).astype(jnp.bfloat16)


def spread(thick_row, layers):
    rows = lax.broadcasted_iota(jnp.int32, (layers, layers), 0)
    cols = lax.broadcasted_iota(jnp.int32, (layers, layers), 1)
    grid = jnp.broadcast_to(thick_row, (layers, layers))
    column = jnp.sum(jnp.where(rows == cols, grid, 0.0), axis=1, keepdims=True)
    return jnp.broadcast_to(column, (layers, LANES))


def onehot_of(row):
    ids = lax.broadcasted_iota(jnp.int32, (SUB, LANES), 0)
    return jnp.where(ids == row, 1.0, 0.0).astype(jnp.bfloat16)


def nt_dot(a, b):
    return lax.dot_general(
        a, b, (((1,), (1,)), ((), ())), preferred_element_type=jnp.float32
    )


def local_kernel(
    pressure, conduct, sat_new, sat_old, porosity, storage, et_rate, thick, labels, outlet,
    partial, balance, edges, peak,
    p_buf, k_buf, n_buf, o_buf, r_buf, s_buf, e_buf, depth, carry, sums, lhs, hot, total, sems,
):
    layers, cx, cy = pressure.shape
    chunks = cx // STEP
    first = ((pressure, p_buf), (conduct, k_buf))
    rest = ((sat_new, n_buf), (sat_old, o_buf), (porosity, r_buf), (storage, s_buf), (et_rate, e_buf))
    pairs = first + rest

    def fetch(chunk, which):
        for a in which:
            source, target = pairs[a]
            for i in range(STEP):
                x = chunk * STEP + i
                pltpu.make_async_copy(source.at[:, x, :], target.at[x], sems.at[a, chunk]).start()

    def wait(chunk, which):
        for a in which:
            target = pairs[a][1].at[pl.ds(chunk * STEP, STEP)]
            pltpu.make_async_copy(target, target, sems.at[a, chunk]).wait()

    fetch(0, (0, 1))
    for chunk in range(chunks):
        if chunk + 1 < chunks:
            fetch(chunk + 1, (0, 1))
        fetch(chunk, range(2, 7))

    p_buf[cx] = jnp.zeros((layers, cy), jnp.float32)
    k_buf[cx] = jnp.zeros((layers, cy), jnp.float32)
    depth[...] = spread(thick[...], layers)
    carry[...] = jnp.zeros_like(carry)
    total[...] = jnp.zeros_like(total)
    peak[...] = jnp.zeros_like(peak)
    sums[...] = jnp.zeros_like(sums)
    edges[:, 2] = jnp.zeros((2, layers, cy), jnp.float32)
    lane = lax.broadcasted_iota(jnp.int32, (ZBLOCK, cy), 1)
    quarter = 4 * layers
    wait(0, (0, 1))

    def fold(value):
        return jnp.sum(value.reshape(ZBLOCK // 8, 8, cy), axis=0)

    def body(chunk, _):
        @pl.when(chunk + 1 < chunks)
        def _():
            wait(chunk + 1, (0, 1))

        wait(chunk, range(2, 7))
        for sub in range(STEP // GROUP):
            for zi in range(layers // ZBLOCK):
                zs = pl.ds(zi * ZBLOCK, ZBLOCK)
                before = carry[zs]
                d = depth[zs]
                biggest = peak[...]
                for i in range(GROUP):
                    x = chunk * STEP + sub * GROUP + i
                    p = p_buf[x, zs]
                    k = k_buf[x, zs]
                    ahead = flow(p, k, p_buf[x + 1, zs], k_buf[x + 1, zs])
                    side = flow(p, k, pltpu.roll(p, cy - 1, 1), pltpu.roll(k, cy - 1, 1))
                    side = jnp.where(lane < cy - 1, side, 0.0)
                    flux = d * (ahead - before + side - pltpu.roll(side, 1, 1))
                    before = ahead
                    mine = (lane >> 1) == x
                    edges[0, 2, zs] = jnp.where(mine, pltpu.roll(p, 2 * x + 1, 1), edges[0, 2, zs])
                    edges[1, 2, zs] = jnp.where(mine, pltpu.roll(k, 2 * x + 1, 1), edges[1, 2, zs])
                    new = n_buf[x, zs]
                    delta = new - o_buf[x, zs]
                    por = r_buf[x, zs]
                    water = d * new * (por + s_buf[x, zs] * p)
                    change = d * por * delta
                    uptake = d * e_buf[x, zs]
                    biggest = jnp.maximum(
                        biggest, jnp.max(jnp.abs(delta).reshape(ZBLOCK // 8, 8, cy), axis=0)
                    )
                    gate = outlet[pl.ds(x, 1), :].astype(jnp.float32)
                    cols = pl.ds(i * cy, cy)
                    for q, (field, kept) in enumerate(
                        ((water, water), (change, change), (uptake, uptake), (flux, flux * gate))
                    ):
                        sums[q, x] += fold(field)
                        high, low = split(kept)
                        row = q * layers + zi * ZBLOCK
                        lhs[sub, pl.ds(row, ZBLOCK), cols] = high
                        lhs[sub, pl.ds(quarter + row, ZBLOCK), cols] = low
                carry[zs] = before
                peak[...] = biggest
            for i in range(GROUP):
                x = chunk * STEP + sub * GROUP + i
                hot[sub, :, pl.ds(i * cy, cy)] = onehot_of(labels[pl.ds(x, 1), :])
            out = nt_dot(lhs[sub], hot[sub])
            total[...] += out[:quarter] + out[quarter:]
        return 0

    lax.fori_loop(0, chunks, body, 0)
    for c in range(SUB // LANES):
        partial[pl.ds(c * quarter, quarter)] = total[:, pl.ds(c * LANES, LANES)]
    for q in range(4):
        balance[q] = jnp.sum(sums[q], axis=1)
    for a, buf in enumerate((p_buf, k_buf)):
        edges[a, 0] = buf[0]
        edges[a, 1] = buf[cx - 1]


def stages_of(n1, n2):
    found = []
    if n1 % 2 == 0 and n1 > 2:
        found += [("gx", 1, 2), ("gx", 2, n1 // 2)]
    else:
        found += [("gx", 1, n1)]
    return found + [("gy", 1, n2)]


def shared_kernel(
    n1, n2, scale,
    partial, balance_in, edges, peak_in, thick, labels, outlet,
    totals, balance, peak,
    halo, work, *rest,
):
    stages = stages_of(n1, n2)
    count = len(stages)
    slots = rest[:count]
    blocks = rest[count : 2 * count]
    tiles = rest[2 * count : 3 * count]
    tops, full, halo_send, halo_recv, send, recv, tile_send, tile_recv, back_send, back_recv = rest[3 * count :]
    gx = lax.axis_index("gx")
    gy = lax.axis_index("gy")
    layers = edges.shape[2]
    cx = labels.shape[0]
    cy = labels.shape[1]
    quarter = 4 * layers

    barrier = pltpu.get_barrier_semaphore()
    for axis, me, n in (("gx", gx, n1), ("gy", gy, n2)):
        for j in range(1, n):
            pl.semaphore_signal(barrier, inc=1, device_id={axis: lax.rem(me + j, n)}, device_id_type=MESH)
    pl.semaphore_wait(barrier, n1 + n2 - 2)

    copies = []
    for slot, (axis, me, n, hop, which) in enumerate(
        (("gx", gx, n1, 1, 1), ("gx", gx, n1, n1 - 1, 0), ("gy", gy, n2, 1, 2), ("gy", gy, n2, n2 - 1, 2))
    ):
        copy = pltpu.make_async_remote_copy(
            src_ref=edges.at[:, which],
            dst_ref=halo.at[slot],
            send_sem=halo_send.at[slot],
            recv_sem=halo_recv.at[slot],
            device_id={axis: lax.rem(me + hop, n)},
            device_id_type=MESH,
        )
        copy.start()
        copies.append(copy)

    depth = spread(thick[...], layers)
    lane = lax.broadcasted_iota(jnp.int32, (layers, cy), 1)
    place_x = lax.broadcasted_iota(jnp.int32, (cx, cy), 0)
    place_c = lax.broadcasted_iota(jnp.int32, (cx, cy), 1)

    def packed(grid):
        top = jnp.broadcast_to(grid[:, cy - 1 :], (cx, cy))
        low = jnp.broadcast_to(grid[:, :1], (cx, cy))
        spot = jnp.where(place_c == 2 * place_x, top, 0) + jnp.where(place_c == 2 * place_x + 1, low, 0)
        return jnp.sum(spot, axis=0, keepdims=True)

    work[...] = partial[...]
    gates = outlet[...].astype(jnp.float32)
    names = labels[...].astype(jnp.float32)
    side_names = packed(names).astype(jnp.int32)
    side_gates = packed(gates)
    hot = jnp.concatenate(
        [onehot_of(labels[pl.ds(0, 1), :]), onehot_of(labels[pl.ds(cx - 1, 1), :]), onehot_of(side_names)], axis=1
    )

    for copy in copies:
        copy.wait()
    inside = (gx > 0, gx < n1 - 1, gy > 0, gy < n2 - 1)
    open_ = [jnp.where(flag, 1.0, 0.0) for flag in inside]
    near_p = [halo[s, 0] for s in range(4)]
    near_k = [halo[s, 1] * open_[s] for s in range(4)]
    low = depth * flow(edges[0, 0], edges[1, 0], near_p[0], near_k[0])
    high = depth * flow(edges[0, 1], edges[1, 1], near_p[1], near_k[1])
    even = (lane & 1) == 0
    side_p = jnp.where(even, pltpu.roll(near_p[3], cy - 1, 1), pltpu.roll(near_p[2], 1, 1))
    side_k = jnp.where(even, pltpu.roll(near_k[3], cy - 1, 1), pltpu.roll(near_k[2], 1, 1))
    own_k = edges[1, 2]
    own_k = jnp.where(lane < 2 * cx, own_k, 1.0)
    side = depth * flow(edges[0, 2], own_k, side_p, side_k)
    side = jnp.where(lane < 2 * cx, side, 0.0)
    extra = jnp.concatenate(
        [low * gates[:1], high * gates[cx - 1 :], side * side_gates], axis=1
    )
    up, down = split(extra)
    out = nt_dot(jnp.concatenate([up, down], axis=0), hot)
    out = out[:layers] + out[layers:]
    for c in range(SUB // LANES):
        work[pl.ds(c * quarter + 3 * layers, layers)] += out[:, c * LANES : (c + 1) * LANES]

    current = work
    rows = SUB // LANES * quarter
    base = 0
    pending = []
    tops[0] = peak_in[...]
    for s, (axis, stride, size) in enumerate(stages):
        me = gx if axis == "gx" else gy
        spot = lax.rem(me // stride, size)
        part = rows // size
        step_copies = []
        for j in range(1, size):
            there = lax.rem(spot + j, size)
            target = me + (there - spot) * stride
            begin = pl.multiple_of(there * part, 8)
            copy = pltpu.make_async_remote_copy(
                src_ref=current.at[pl.ds(begin, part)],
                dst_ref=slots[s].at[j - 1],
                send_sem=send.at[s, j - 1],
                recv_sem=recv.at[s, j - 1],
                device_id={axis: target},
                device_id_type=MESH,
            )
            copy.start()
            step_copies.append(copy)
            copy = pltpu.make_async_remote_copy(
                src_ref=tops.at[s],
                dst_ref=tiles[s].at[j - 1],
                send_sem=tile_send.at[s, j - 1],
                recv_sem=tile_recv.at[s, j - 1],
                device_id={axis: target},
                device_id_type=MESH,
            )
            copy.start()
            step_copies.append(copy)
        for copy in step_copies:
            copy.wait_recv()
        pending += step_copies
        mine = pl.multiple_of(spot * part, 8)
        value = current[pl.ds(mine, part)]
        top = tops[s]
        for j in range(size - 1):
            value = value + slots[s][j]
            top = jnp.maximum(top, tiles[s][j])
        tops[s + 1] = top
        base = base + spot * part
        rows = part
        if s + 1 < count:
            blocks[s][...] = value
            current = blocks[s]
        else:
            full[pl.ds(pl.multiple_of(base, 8), part)] = value * scale

    for s in range(count - 1, -1, -1):
        axis, stride, size = stages[s]
        me = gx if axis == "gx" else gy
        spot = lax.rem(me // stride, size)
        held = full.at[pl.ds(pl.multiple_of(base, 8), rows)]
        step_copies = []
        for j in range(1, size):
            there = lax.rem(spot + j, size)
            copy = pltpu.make_async_remote_copy(
                src_ref=held,
                dst_ref=held,
                send_sem=back_send.at[s, j - 1],
                recv_sem=back_recv.at[s, j - 1],
                device_id={axis: me + (there - spot) * stride},
                device_id_type=MESH,
            )
            copy.start()
            step_copies.append(copy)
        if s == count - 1:
            sum_low = jnp.sum(low, axis=0, keepdims=True)
            sum_high = jnp.sum(high, axis=0, keepdims=True)
            sum_side = jnp.broadcast_to(jnp.sum(side, axis=0, keepdims=True), (cx, cy))
            column_top = jnp.sum(jnp.where(place_c == 2 * place_x, sum_side, 0.0), axis=1, keepdims=True)
            column_low = jnp.sum(jnp.where(place_c == 2 * place_x + 1, sum_side, 0.0), axis=1, keepdims=True)
            more = jnp.where(place_c == cy - 1, column_top, 0.0) + jnp.where(place_c == 0, column_low, 0.0)
            more = more + jnp.where(place_x == 0, sum_low, 0.0) + jnp.where(place_x == cx - 1, sum_high, 0.0)
            balance[pl.ds(0, 3)] = balance_in[pl.ds(0, 3)]
            balance[3] = balance_in[3] + more
            best = jnp.max(jnp.max(tops[count], axis=0, keepdims=True), axis=1, keepdims=True)
            peak[...] = best
        for copy in step_copies:
            copy.wait_recv()
        pending += step_copies
        base = base - spot * rows
        rows = rows * size
    for c in range(SUB // LANES):
        for q in range(4):
            totals[q, :, pl.ds(c * LANES, LANES)] = full[pl.ds(c * quarter + q * layers, layers)]
    for copy in pending:
        copy.wait_send()


def on_device(
    n1, n2,
    sat_new, sat_old, porosity, spec_storage, pressure, conduct, et_rate, thickness, labels, outlet
):
    layers, cx, cy = sat_new.shape
    quarter = 4 * layers
    f32 = jnp.float32
    vmem = pl.BlockSpec(memory_space=pltpu.VMEM)
    hbm = pl.BlockSpec(memory_space=pl.ANY)
    rows = SUB // LANES * quarter
    thick = thickness.reshape(1, layers)
    slab = pltpu.VMEM((cx, layers, cy), f32)
    slab1 = pltpu.VMEM((cx + 1, layers, cy), f32)
    partial, balance, edges, peak = pl.pallas_call(
        local_kernel,
        out_shape=(
            jax.ShapeDtypeStruct((rows, LANES), f32),
            jax.ShapeDtypeStruct((4, cx, cy), f32),
            jax.ShapeDtypeStruct((2, 3, layers, cy), f32),
            jax.ShapeDtypeStruct((8, cy), f32),
        ),
        in_specs=[hbm] * 7 + [vmem] * 3,
        out_specs=(vmem,) * 4,
        scratch_shapes=[slab1, slab1] + [slab] * 5 + [
            pltpu.VMEM((layers, cy), f32),
            pltpu.VMEM((layers, cy), f32),
            pltpu.VMEM((4, cx, 8, cy), f32),
            pltpu.VMEM((STEP // GROUP, 2 * quarter, GROUP * cy), jnp.bfloat16),
            pltpu.VMEM((STEP // GROUP, SUB, GROUP * cy), jnp.bfloat16),
            pltpu.VMEM((quarter, SUB), f32),
            pltpu.SemaphoreType.DMA((7, cx // STEP)),
        ],
        compiler_params=pltpu.CompilerParams(vmem_limit_bytes=VMEM_LIMIT),
        name="local",
    )(pressure, conduct, sat_new, sat_old, porosity, spec_storage, et_rate, thick, labels, outlet)

    stages = stages_of(n1, n2)
    count = len(stages)
    widest = max(size for _, _, size in stages) - 1
    left = rows
    slots, blocks, tiles = [], [], []
    for _, _, size in stages:
        left //= size
        slots.append(pltpu.VMEM((size - 1, left, LANES), f32))
        blocks.append(pltpu.VMEM((left, LANES), f32))
        tiles.append(pltpu.VMEM((size - 1, 8, LANES), f32))
    dma = pltpu.SemaphoreType.DMA
    scale = layers * SUB / (cx * n1 * cy * n2)
    totals, balance, peak = pl.pallas_call(
        functools.partial(shared_kernel, n1, n2, scale),
        out_shape=(
            jax.ShapeDtypeStruct((4, layers, SUB), f32),
            jax.ShapeDtypeStruct((4, cx, cy), f32),
            jax.ShapeDtypeStruct((1, 1), f32),
        ),
        in_specs=[vmem] * 7,
        out_specs=(vmem,) * 3,
        scratch_shapes=[
            pltpu.VMEM((4, 2, layers, cy), f32),
            pltpu.VMEM((rows, LANES), f32),
            *slots, *blocks, *tiles,
            pltpu.VMEM((count + 1, 8, LANES), f32),
            pltpu.VMEM((rows, LANES), f32),
            dma((4,)), dma((4,)),
        ] + [dma((count, widest))] * 6,
        compiler_params=pltpu.CompilerParams(
            collective_id=0, has_side_effects=True, vmem_limit_bytes=32 * 1024 * 1024
        ),
        name="shared",
    )(partial, balance, edges, peak, thick, labels, outlet)
    return totals, balance, peak[0, 0]


def solution(mesh):
    columns = P(None, "gx", "gy")
    in_specs = (columns,) * 7 + (P(), P("gx", "gy"), P("gx", "gy"))
    out_specs = (P(), columns, P())
    body = functools.partial(on_device, mesh.shape["gx"], mesh.shape["gy"])
    return jax.shard_map(
        body, mesh=mesh, in_specs=in_specs, out_specs=out_specs, check_vma=False
    )
```

profile of v0, /device:TPU:0, one launch (start us, length us, event | category | flops | bytes accessed | tf_op | source)
XLA Modules:
  0.0 52.0 jit_solution(13247928654541849224)
XLA Ops:
  0.6 0.0 copy-start.2
  0.6 0.0 copy-start.3
  0.7 0.0 copy-start.6
  0.7 13.9 %local.1 = (f32[1024,128]{1,0:T(8,128)}, f32[4,64,128]{2,1,0:T(8,128)}, f32[2,3,64,128]{3,2,1,0:T(8,128)}, f32[8,128]{1,0:T(8,128)}) custom-call(f32[64,64,128]{2,1,0:T(8,128)} %pressure.1, f32[64,64,128]{2,1,0:T(8,128)} %conduct.1, f32[64,64,128]{2,1,0:T(8,128)} %sat_new.1, f32[64,64,128]{2,1,0:T(8,128)} %sat_old.1, f32[64,64,128]{2,1,0:T(8,128)} %porosity.1, ...), custom_call_target="tpu_custom_call" | custom-call | tf_op jit(solution)/shard_map/local/pallas_call | solution.py:353
  14.6 0.0 copy-done.2
  14.6 0.0 copy-done.3
  14.6 0.0 copy-done.6
  14.6 0.0 copy-start
  14.6 1.0 %copy-done = f32[1024,128]{1,0:T(8,128)S(1)} copy-done((f32[1024,128]{1,0:T(8,128)S(1)}, f32[1024,128]{1,0:T(8,128)}, u32[]{:S(2)}) %copy-start) | copy-done | bytes 524312
  15.7 0.0 copy-start.1
  15.7 0.9 %copy-done.1 = f32[2,3,64,128]{3,2,1,0:T(8,128)S(1)} copy-done((f32[2,3,64,128]{3,2,1,0:T(8,128)S(1)}, f32[2,3,64,128]{3,2,1,0:T(8,128)}, u32[]{:S(2)}) %copy-start.1) | copy-done | bytes 196632
  16.6 0.0 copy-start.4
  16.6 0.9 %copy-done.4 = f32[4,64,128]{2,1,0:T(8,128)S(1)} copy-done((f32[4,64,128]{2,1,0:T(8,128)S(1)}, f32[4,64,128]{2,1,0:T(8,128)}, u32[]{:S(2)}) %copy-start.4) | copy-done | bytes 131096
  17.5 0.0 copy-start.5
  17.5 0.7 %copy-done.5 = f32[8,128]{1,0:T(8,128)S(1)} copy-done((f32[8,128]{1,0:T(8,128)S(1)}, f32[8,128]{1,0:T(8,128)}, u32[]{:S(2)}) %copy-start.5) | copy-done | bytes 4120
  18.2 30.6 %shared.1 = (f32[4,64,512]{2,1,0:T(8,128)S(1)}, f32[4,64,128]{2,1,0:T(8,128)S(1)}, f32[1,1]{1,0:T(1,128)}) custom-call(f32[1024,128]{1,0:T(8,128)S(1)} %copy-done, f32[4,64,128]{2,1,0:T(8,128)S(1)} %copy-done.4, f32[2,3,64,128]{3,2,1,0:T(8,128)S(1)} %copy-done.1, f32[8,128]{1,0:T(8,128)S(1)} %copy-done.5, f32[1,64]{1,0:T(1,128)S(1)} %bitcast.3, ...), custom_call_target="tpu_custom_call" | custom-call | tf_op jit(solution)/shard_map/shared/pallas_call | solution.py:388
  48.7 0.8 %copy.16 = f32[4,64,512]{2,1,0:T(8,128)} copy(f32[4,64,512]{2,1,0:T(8,128)S(1)} %get-tuple-element.20) | data formatting | bytes 1048576
  49.5 0.7 %copy.17 = f32[4,64,128]{2,1,0:T(8,128)} copy(f32[4,64,128]{2,1,0:T(8,128)S(1)} %get-tuple-element.21) | data formatting | bytes 262144
Async XLA Ops:
  0.6 14.0 %copy-start.2 = (s32[64,128]{1,0:T(8,128)S(1)}, s32[64,128]{1,0:T(8,128)}, u32[]{:S(2)}) copy-start(s32[64,128]{1,0:T(8,128)} %labels.3) | copy-start | bytes 98308
  0.6 14.0 %copy-start.3 = (s32[64,128]{1,0:T(8,128)S(1)}, s32[64,128]{1,0:T(8,128)}, u32[]{:S(2)}) copy-start(s32[64,128]{1,0:T(8,128)} %outlet.3) | copy-start | bytes 98308
  0.7 14.0 %copy-start.6 = (f32[64]{0:T(128)S(1)}, f32[64]{0:T(128)}, u32[]{:S(2)}) copy-start(f32[64]{0:T(128)} %param.17) | copy-start | bytes 772
  14.6 1.0 %copy-start = (f32[1024,128]{1,0:T(8,128)S(1)}, f32[1024,128]{1,0:T(8,128)}, u32[]{:S(2)}) copy-start(f32[1024,128]{1,0:T(8,128)} %get-tuple-element.10.partial) | copy-start | bytes 1572868
  15.7 0.9 %copy-start.1 = (f32[2,3,64,128]{3,2,1,0:T(8,128)S(1)}, f32[2,3,64,128]{3,2,1,0:T(8,128)}, u32[]{:S(2)}) copy-start(f32[2,3,64,128]{3,2,1,0:T(8,128)} %get-tuple-element.12.edges) | copy-start | bytes 589828
  16.6 0.9 %copy-start.4 = (f32[4,64,128]{2,1,0:T(8,128)S(1)}, f32[4,64,128]{2,1,0:T(8,128)}, u32[]{:S(2)}) copy-start(f32[4,64,128]{2,1,0:T(8,128)} %get-tuple-element.11.balance_in) | copy-start | bytes 393220
  17.5 0.7 %copy-start.5 = (f32[8,128]{1,0:T(8,128)S(1)}, f32[8,128]{1,0:T(8,128)}, u32[]{:S(2)}) copy-start(f32[8,128]{1,0:T(8,128)} %get-tuple-element.13.peak_in) | copy-start | bytes 12292
where the time goes:
time: 52.3 us; the launch traced here: 52 us
  Pallas kernels  44.5 us (85%)
  local copies, waits for them, and re-layouts  5.01 us (10%)
  between operations  2.52 us (5%)
    pallas_call x1, Pallas kernels, on_device(): pl.pallas_call(functools.partial(shared_kernel, n1, n2, scale), out_shape...  30.6 us
    pallas_call x1, Pallas kernels, on_device(): pl.pallas_call(local_kernel, out_shape=(jax.ShapeDtypeStruct((rows, LANES...  13.9 us
    unnamed x16, local copies, waits for them, and re-layouts  5.01 us

commit v1 on v0

--- a/solution.py
+++ b/solution.py
@@ -13,7 +13,7 @@
 GROUP = 4
 ZBLOCK = 32
 MESH = pl.DeviceIdType.MESH
-VMEM_LIMIT = 60 * 1024 * 1024
+VMEM_LIMIT = 48 * 512 * 1024
 
 
 def flow(p, k, pn, kn):
@@ -141,8 +141,11 @@
         return 0
 
     lax.fori_loop(0, chunks, body, 0)
-    for c in range(SUB // LANES):
-        partial[pl.ds(c * quarter, quarter)] = total[:, pl.ds(c * LANES, LANES)]
+    strips = SUB // LANES
+    for q in range(4):
+        for c in range(strips):
+            block = pl.ds((q * strips + c) * layers, layers)
+            partial[block] = total[pl.ds(q * layers, layers), pl.ds(c * LANES, LANES)]
     for q in range(4):
         balance[q] = jnp.sum(sums[q], axis=1)
     for a, buf in enumerate((p_buf, k_buf)):
@@ -160,7 +163,7 @@
 
 
 def shared_kernel(
-    n1, n2, scale,
+    n1, n2, slices, scale,
     partial, balance_in, edges, peak_in, thick, labels, outlet,
     totals, balance, peak,
     halo, work, *rest,
@@ -176,8 +179,61 @@
     layers = edges.shape[2]
     cx = labels.shape[0]
     cy = labels.shape[1]
-    quarter = 4 * layers
-
+    strips = SUB // LANES
+    length = 4 * strips * layers // slices
+    last = slices - 1
+    places = []
+    for axis, stride, size in stages:
+        me = gx if axis == "gx" else gy
+        places.append((axis, me, stride, size, lax.rem(me // stride, size)))
+    parts = []
+    for _, _, size in stages:
+        parts.append((parts[-1] if parts else length) // size)
+    pending = []
+
+    def sources(s):
+        if s == 0:
+            return [partial.at[pl.ds(k * length, length)] for k in range(last)] + [work]
+        return [blocks[s - 1].at[k] for k in range(slices)]
+
+    def scatter(s, k):
+        axis, me, stride, size, spot = places[s]
+        part = parts[s]
+        found = []
+        for j in range(1, size):
+            there = lax.rem(spot + j, size)
+            copy = pltpu.make_async_remote_copy(
+                src_ref=sources(s)[k].at[pl.ds(pl.multiple_of(there * part, min(part, 8)), part)],
+                dst_ref=slots[s].at[k, j - 1],
+                send_sem=send.at[s, k, j - 1],
+                recv_sem=recv.at[s, k, j - 1],
+                device_id={axis: me + (there - spot) * stride},
+                device_id_type=MESH,
+            )
+            copy.start()
+            found.append(copy)
+        pending.extend(found)
+        return found
+
+    def exchange(s):
+        axis, me, stride, size, spot = places[s]
+        found = []
+        for j in range(1, size):
+            there = lax.rem(spot + j, size)
+            copy = pltpu.make_async_remote_copy(
+                src_ref=tops.at[s],
+                dst_ref=tiles[s].at[j - 1],
+                send_sem=tile_send.at[s, j - 1],
+                recv_sem=tile_recv.at[s, j - 1],
+                device_id={axis: me + (there - spot) * stride},
+                device_id_type=MESH,
+            )
+            copy.start()
+            found.append(copy)
+        pending.extend(found)
+        return found
+
+    tops[0] = peak_in[...]
     barrier = pltpu.get_barrier_semaphore()
     for axis, me, n in (("gx", gx, n1), ("gy", gy, n2)):
         for j in range(1, n):
@@ -198,6 +254,8 @@
         )
         copy.start()
         copies.append(copy)
+    moving = [scatter(0, k) for k in range(last)]
+    top_moving = exchange(0)
 
     depth = spread(thick[...], layers)
     lane = lax.broadcasted_iota(jnp.int32, (layers, cy), 1)
@@ -210,7 +268,7 @@
         spot = jnp.where(place_c == 2 * place_x, top, 0) + jnp.where(place_c == 2 * place_x + 1, low, 0)
         return jnp.sum(spot, axis=0, keepdims=True)
 
-    work[...] = partial[...]
+    work[...] = partial[pl.ds(last * length, length)]
     gates = outlet[...].astype(jnp.float32)
     names = labels[...].astype(jnp.float32)
     side_names = packed(names).astype(jnp.int32)
@@ -230,8 +288,7 @@
     even = (lane & 1) == 0
     side_p = jnp.where(even, pltpu.roll(near_p[3], cy - 1, 1), pltpu.roll(near_p[2], 1, 1))
     side_k = jnp.where(even, pltpu.roll(near_k[3], cy - 1, 1), pltpu.roll(near_k[2], 1, 1))
-    own_k = edges[1, 2]
-    own_k = jnp.where(lane < 2 * cx, own_k, 1.0)
+    own_k = jnp.where(lane < 2 * cx, edges[1, 2], 1.0)
     side = depth * flow(edges[0, 2], own_k, side_p, side_k)
     side = jnp.where(lane < 2 * cx, side, 0.0)
     extra = jnp.concatenate(
@@ -240,101 +297,91 @@
     up, down = split(extra)
     out = nt_dot(jnp.concatenate([up, down], axis=0), hot)
     out = out[:layers] + out[layers:]
-    for c in range(SUB // LANES):
-        work[pl.ds(c * quarter + 3 * layers, layers)] += out[:, c * LANES : (c + 1) * LANES]
-
-    current = work
-    rows = SUB // LANES * quarter
-    base = 0
-    pending = []
-    tops[0] = peak_in[...]
-    for s, (axis, stride, size) in enumerate(stages):
-        me = gx if axis == "gx" else gy
-        spot = lax.rem(me // stride, size)
-        part = rows // size
-        step_copies = []
-        for j in range(1, size):
-            there = lax.rem(spot + j, size)
-            target = me + (there - spot) * stride
-            begin = pl.multiple_of(there * part, 8)
-            copy = pltpu.make_async_remote_copy(
-                src_ref=current.at[pl.ds(begin, part)],
-                dst_ref=slots[s].at[j - 1],
-                send_sem=send.at[s, j - 1],
-                recv_sem=recv.at[s, j - 1],
-                device_id={axis: target},
-                device_id_type=MESH,
-            )
-            copy.start()
-            step_copies.append(copy)
-            copy = pltpu.make_async_remote_copy(
-                src_ref=tops.at[s],
-                dst_ref=tiles[s].at[j - 1],
-                send_sem=tile_send.at[s, j - 1],
-                recv_sem=tile_recv.at[s, j - 1],
-                device_id={axis: target},
-                device_id_type=MESH,
-            )
-            copy.start()
-            step_copies.append(copy)
-        for copy in step_copies:
-            copy.wait_recv()
-        pending += step_copies
-        mine = pl.multiple_of(spot * part, 8)
-        value = current[pl.ds(mine, part)]
-        top = tops[s]
-        for j in range(size - 1):
-            value = value + slots[s][j]
-            top = jnp.maximum(top, tiles[s][j])
-        tops[s + 1] = top
-        base = base + spot * part
-        rows = part
-        if s + 1 < count:
-            blocks[s][...] = value
-            current = blocks[s]
-        else:
-            full[pl.ds(pl.multiple_of(base, 8), part)] = value * scale
+    begin = length - strips * layers
+    for c in range(strips):
+        work[pl.ds(begin + c * layers, layers)] += out[:, c * LANES : (c + 1) * LANES]
+    moving.append(scatter(0, last))
+
+    for s in range(count):
+        _, _, _, size, spot = places[s]
+        part = parts[s]
+        later = []
+        for k in range(slices):
+            for copy in moving[k]:
+                copy.wait_recv()
+            mine = pl.multiple_of(spot * part, min(part, 8))
+            value = sources(s)[k][pl.ds(mine, part)]
+            for j in range(size - 1):
+                value = value + slots[s][k, j]
+            if s + 1 < count:
+                blocks[s][k] = value
+                later.append(scatter(s + 1, k))
+            else:
+                base = 0
+                for (_, _, _, _, spot_of), part_of in zip(places, parts):
+                    base = base + spot_of * part_of
+                full[pl.ds(pl.multiple_of(k * length + base, min(part, 8)), part)] = value * scale
+                later.append(gather(s, k, base, places, parts, full, back_send, back_recv, pending))
+            if k == 0:
+                for copy in top_moving:
+                    copy.wait_recv()
+                top = tops[s]
+                for j in range(size - 1):
+                    top = jnp.maximum(top, tiles[s][j])
+                tops[s + 1] = top
+                top_moving = exchange(s + 1) if s + 1 < count else []
+        moving = later
+
+    sum_low = jnp.sum(low, axis=0, keepdims=True)
+    sum_high = jnp.sum(high, axis=0, keepdims=True)
+    sum_side = jnp.broadcast_to(jnp.sum(side, axis=0, keepdims=True), (cx, cy))
+    column_top = jnp.sum(jnp.where(place_c == 2 * place_x, sum_side, 0.0), axis=1, keepdims=True)
+    column_low = jnp.sum(jnp.where(place_c == 2 * place_x + 1, sum_side, 0.0), axis=1, keepdims=True)
+    more = jnp.where(place_c == cy - 1, column_top, 0.0) + jnp.where(place_c == 0, column_low, 0.0)
+    more = more + jnp.where(place_x == 0, sum_low, 0.0) + jnp.where(place_x == cx - 1, sum_high, 0.0)
+    balance[pl.ds(0, 3)] = balance_in[pl.ds(0, 3)]
+    balance[3] = balance_in[3] + more
+    peak[...] = jnp.max(jnp.max(tops[count], axis=0, keepdims=True), axis=1, keepdims=True)
 
     for s in range(count - 1, -1, -1):
-        axis, stride, size = stages[s]
-        me = gx if axis == "gx" else gy
-        spot = lax.rem(me // stride, size)
-        held = full.at[pl.ds(pl.multiple_of(base, 8), rows)]
-        step_copies = []
-        for j in range(1, size):
-            there = lax.rem(spot + j, size)
-            copy = pltpu.make_async_remote_copy(
-                src_ref=held,
-                dst_ref=held,
-                send_sem=back_send.at[s, j - 1],
-                recv_sem=back_recv.at[s, j - 1],
-                device_id={axis: me + (there - spot) * stride},
-                device_id_type=MESH,
-            )
-            copy.start()
-            step_copies.append(copy)
-        if s == count - 1:
-            sum_low = jnp.sum(low, axis=0, keepdims=True)
-            sum_high = jnp.sum(high, axis=0, keepdims=True)
-            sum_side = jnp.broadcast_to(jnp.sum(side, axis=0, keepdims=True), (cx, cy))
-            column_top = jnp.sum(jnp.where(place_c == 2 * place_x, sum_side, 0.0), axis=1, keepdims=True)
-            column_low = jnp.sum(jnp.where(place_c == 2 * place_x + 1, sum_side, 0.0), axis=1, keepdims=True)
-            more = jnp.where(place_c == cy - 1, column_top, 0.0) + jnp.where(place_c == 0, column_low, 0.0)
-            more = more + jnp.where(place_x == 0, sum_low, 0.0) + jnp.where(place_x == cx - 1, sum_high, 0.0)
-            balance[pl.ds(0, 3)] = balance_in[pl.ds(0, 3)]
-            balance[3] = balance_in[3] + more
-            best = jnp.max(jnp.max(tops[count], axis=0, keepdims=True), axis=1, keepdims=True)
-            peak[...] = best
-        for copy in step_copies:
-            copy.wait_recv()
-        pending += step_copies
-        base = base - spot * rows
-        rows = rows * size
-    for c in range(SUB // LANES):
-        for q in range(4):
-            totals[q, :, pl.ds(c * LANES, LANES)] = full[pl.ds(c * quarter + q * layers, layers)]
+        base = 0
+        for (_, _, _, _, spot_of), part_of in zip(places[:s], parts[:s]):
+            base = base + spot_of * part_of
+        later = []
+        for k in range(slices):
+            for copy in moving[k]:
+                copy.wait_recv()
+            if s > 0:
+                later.append(gather(s - 1, k, base, places, parts, full, back_send, back_recv, pending))
+            else:
+                for block in range(k * length // layers, (k + 1) * length // layers):
+                    q, c = divmod(block, strips)
+                    totals[q, :, pl.ds(c * LANES, LANES)] = full[pl.ds(block * layers, layers)]
+        moving = later
     for copy in pending:
         copy.wait_send()
+
+
+def gather(s, k, base, places, parts, full, back_send, back_recv, pending):
+    axis, me, stride, size, spot = places[s]
+    part = parts[s]
+    length = parts[0] * places[0][3]
+    held = full.at[pl.ds(pl.multiple_of(k * length + base, min(part, 8)), part)]
+    found = []
+    for j in range(1, size):
+        there = lax.rem(spot + j, size)
+        copy = pltpu.make_async_remote_copy(
+            src_ref=held,
+            dst_ref=held,
+            send_sem=back_send.at[s, k, j - 1],
+            recv_sem=back_recv.at[s, k, j - 1],
+            device_id={axis: me + (there - spot) * stride},
+            device_id_type=MESH,
+        )
+        copy.start()
+        found.append(copy)
+    pending.extend(found)
+    return found
 
 
 def on_device(
@@ -345,7 +392,7 @@
     quarter = 4 * layers
     f32 = jnp.float32
     vmem = pl.BlockSpec(memory_space=pltpu.VMEM)
-    hbm = pl.BlockSpec(memory_space=pl.ANY)
+    hbm = pl.BlockSpec(memory_space=pltpu.HBM)
     rows = SUB // LANES * quarter
     thick = thickness.reshape(1, layers)
     slab = pltpu.VMEM((cx, layers, cy), f32)
@@ -371,22 +418,23 @@
         ],
         compiler_params=pltpu.CompilerParams(vmem_limit_bytes=VMEM_LIMIT),
         name="local",
-    )(pressure, conduct, sat_new, sat_old, porosity, spec_storage, et_rate, thick, labels, outlet)
+    )(*[pltpu.with_memory_space_constraint(v, pltpu.HBM) for v in (pressure, conduct, sat_new, sat_old, porosity, spec_storage, et_rate)], thick, labels, outlet)
 
     stages = stages_of(n1, n2)
     count = len(stages)
     widest = max(size for _, _, size in stages) - 1
-    left = rows
+    slices = max(1, min(4, rows // (8 * n1 * n2)))
+    left = rows // slices
     slots, blocks, tiles = [], [], []
     for _, _, size in stages:
         left //= size
-        slots.append(pltpu.VMEM((size - 1, left, LANES), f32))
-        blocks.append(pltpu.VMEM((left, LANES), f32))
+        slots.append(pltpu.VMEM((slices, size - 1, left, LANES), f32))
+        blocks.append(pltpu.VMEM((slices, left, LANES), f32))
         tiles.append(pltpu.VMEM((size - 1, 8, LANES), f32))
     dma = pltpu.SemaphoreType.DMA
     scale = layers * SUB / (cx * n1 * cy * n2)
     totals, balance, peak = pl.pallas_call(
-        functools.partial(shared_kernel, n1, n2, scale),
+        functools.partial(shared_kernel, n1, n2, slices, scale),
         out_shape=(
             jax.ShapeDtypeStruct((4, layers, SUB), f32),
             jax.ShapeDtypeStruct((4, cx, cy), f32),
@@ -396,14 +444,17 @@
         out_specs=(vmem,) * 3,
         scratch_shapes=[
             pltpu.VMEM((4, 2, layers, cy), f32),
-            pltpu.VMEM((rows, LANES), f32),
+            pltpu.VMEM((rows // slices, LANES), f32),
             *slots, *blocks, *tiles,
             pltpu.VMEM((count + 1, 8, LANES), f32),
             pltpu.VMEM((rows, LANES), f32),
             dma((4,)), dma((4,)),
-        ] + [dma((count, widest))] * 6,
+            dma((count, slices, widest)), dma((count, slices, widest)),
+            dma((count, widest)), dma((count, widest)),
+            dma((count, slices, widest)), dma((count, slices, widest)),
+        ],
         compiler_params=pltpu.CompilerParams(
-            collective_id=0, has_side_effects=True, vmem_limit_bytes=32 * 1024 * 1024
+            collective_id=0, has_side_effects=True, vmem_limit_bytes=16 * 1024 * 1024
         ),
         name="shared",
     )(partial, balance, edges, peak, thick, labels, outlet)

time: 52.3 us -> 47.6 us (0.910)
  Pallas kernels: 44.5 us -> 41.3 us
  local copies, waits for them, and re-layouts: 5.01 us -> 3.61 us
    pallas_call x1, Pallas kernels: 13.9 us -> 12.3 us  [on_device(): pl.pallas_call(local_kernel, out_shape=(jax.ShapeDtypeStruct((rows, LANES...]
    pallas_call x1, Pallas kernels: 30.6 us -> 29 us  [on_device(): pl.pallas_call(functools.partial(shared_kernel, n1, n2, slices, scale), o...]
    unnamed x16 -> x8, local copies, waits for them, and re-layouts: 5.01 us -> 3.61 us
where the time goes in v1:
time: 47.6 us; the launch traced here: 47.3 us
  Pallas kernels  41.3 us (87%)
  local copies, waits for them, and re-layouts  3.61 us (8%)
  between operations  2.41 us (5%)
    pallas_call x1, Pallas kernels, on_device(): pl.pallas_call(functools.partial(shared_kernel, n1, n2, slices, scale), o...  29 us
    pallas_call x1, Pallas kernels, on_device(): pl.pallas_call(local_kernel, out_shape=(jax.ShapeDtypeStruct((rows, LANES...  12.3 us
    unnamed x8, local copies, waits for them, and re-layouts  3.61 us

profile of v1, /device:TPU:0, one launch (start us, length us, event | category | flops | bytes accessed | tf_op | source)
XLA Modules:
  0.0 47.3 jit_solution(665709145636853949)
XLA Ops:
  0.6 0.0 copy-start
  0.6 0.7 %copy-done = s32[64,128]{1,0:T(8,128)S(1)} copy-done((s32[64,128]{1,0:T(8,128)S(1)}, s32[64,128]{1,0:T(8,128)}, u32[]{:S(2)}) %copy-start) | copy-done | bytes 32792
  1.4 0.0 copy-start.1
  1.4 0.8 %copy-done.1 = s32[64,128]{1,0:T(8,128)S(1)} copy-done((s32[64,128]{1,0:T(8,128)S(1)}, s32[64,128]{1,0:T(8,128)}, u32[]{:S(2)}) %copy-start.1) | copy-done | bytes 32792
  2.2 0.0 copy-start.2
  2.2 0.7 %copy-done.2 = f32[64]{0:T(128)S(1)} copy-done((f32[64]{0:T(128)S(1)}, f32[64]{0:T(128)}, u32[]{:S(2)}) %copy-start.2) | copy-done | bytes 280
  2.8 12.3 %local.1 = (f32[1024,128]{1,0:T(8,128)S(1)}, f32[4,64,128]{2,1,0:T(8,128)S(1)}, f32[2,3,64,128]{3,2,1,0:T(8,128)S(1)}, f32[8,128]{1,0:T(8,128)S(1)}) custom-call(f32[64,64,128]{2,1,0:T(8,128)} %pressure.1, f32[64,64,128]{2,1,0:T(8,128)} %conduct.1, f32[64,64,128]{2,1,0:T(8,128)} %sat_new.1, f32[64,64,128]{2,1,0:T(8,128)} %sat_old.1, ...), custom_call_target="tpu_custom_call" | custom-call | tf_op jit(solution)/shard_map/local/pallas_call | solution.py:400
  15.1 29.0 %shared.1 = (f32[4,64,512]{2,1,0:T(8,128)S(1)}, f32[4,64,128]{2,1,0:T(8,128)S(1)}, f32[1,1]{1,0:T(1,128)}) custom-call(f32[1024,128]{1,0:T(8,128)S(1)} %get-tuple-element.10.partial, f32[4,64,128]{2,1,0:T(8,128)S(1)} %get-tuple-element.11.balance_in, f32[2,3,64,128]{3,2,1,0:T(8,128)S(1)} %get-tuple-element.12.edges, f32[8,128]{1,0:T(8,128)S(1)} %get-tuple-element.13.peak_in, ...), custom_call_target="tpu_custom_call" | custom-call | tf_op jit(solution)/shard_map/shared/pallas_call | solution.py:436
  44.1 0.8 %copy.16 = f32[4,64,512]{2,1,0:T(8,128)} copy(f32[4,64,512]{2,1,0:T(8,128)S(1)} %get-tuple-element.20) | data formatting | bytes 1048576
  44.9 0.7 %copy.17 = f32[4,64,128]{2,1,0:T(8,128)} copy(f32[4,64,128]{2,1,0:T(8,128)S(1)} %get-tuple-element.21) | data formatting | bytes 262144
Async XLA Ops:
  0.6 0.8 %copy-start = (s32[64,128]{1,0:T(8,128)S(1)}, s32[64,128]{1,0:T(8,128)}, u32[]{:S(2)}) copy-start(s32[64,128]{1,0:T(8,128)} %labels.3) | copy-start | bytes 98308
  1.4 0.8 %copy-start.1 = (s32[64,128]{1,0:T(8,128)S(1)}, s32[64,128]{1,0:T(8,128)}, u32[]{:S(2)}) copy-start(s32[64,128]{1,0:T(8,128)} %outlet.3) | copy-start | bytes 98308
  2.2 0.7 %copy-start.2 = (f32[64]{0:T(128)S(1)}, f32[64]{0:T(128)}, u32[]{:S(2)}) copy-start(f32[64]{0:T(128)} %param.17) | copy-start | bytes 772

commit v2 on v1

--- a/solution.py
+++ b/solution.py
@@ -418,7 +418,7 @@
         ],
         compiler_params=pltpu.CompilerParams(vmem_limit_bytes=VMEM_LIMIT),
         name="local",
-    )(*[pltpu.with_memory_space_constraint(v, pltpu.HBM) for v in (pressure, conduct, sat_new, sat_old, porosity, spec_storage, et_rate)], thick, labels, outlet)
+    )(*[pltpu.with_memory_space_constraint(v, pltpu.HBM) for v in (pressure, conduct, sat_new, sat_old, porosity, spec_storage, et_rate, thick, labels, outlet)])
 
     stages = stages_of(n1, n2)
     count = len(stages)

time: 47.6 us -> 46.2 us (0.971)
  local copies, waits for them, and re-layouts: 3.61 us -> 1.46 us
  Pallas kernels: 41.3 us -> 42 us
    unnamed x8, local copies, waits for them, and re-layouts: 3.61 us -> 1.46 us
    pallas_call x1, Pallas kernels: 12.3 us -> 13.1 us  [on_device(): pl.pallas_call(local_kernel, out_shape=(jax.ShapeDtypeStruct((rows, LANES...]
where the time goes in v2:
time: 46.2 us; the launch traced here: 46 us
  Pallas kernels  42 us (91%)
  between operations  2.45 us (5%)
  local copies, waits for them, and re-layouts  1.46 us (3%)
    pallas_call x1, Pallas kernels, on_device(): pl.pallas_call(functools.partial(shared_kernel, n1, n2, slices, scale), o...  29 us
    pallas_call x1, Pallas kernels, on_device(): pl.pallas_call(local_kernel, out_shape=(jax.ShapeDtypeStruct((rows, LANES...  13.1 us
    unnamed x8, local copies, waits for them, and re-layouts  1.46 us

profile of v2, /device:TPU:0, one launch (start us, length us, event | category | flops | bytes accessed | tf_op | source)
XLA Modules:
  0.0 46.0 jit_solution(5670863069844647988)
XLA Ops:
  0.6 0.0 copy-start
  0.6 0.0 copy-start.1
  0.7 0.0 copy-start.2
  0.7 13.1 %local.1 = (f32[1024,128]{1,0:T(8,128)S(1)}, f32[4,64,128]{2,1,0:T(8,128)S(1)}, f32[2,3,64,128]{3,2,1,0:T(8,128)S(1)}, f32[8,128]{1,0:T(8,128)S(1)}) custom-call(f32[64,64,128]{2,1,0:T(8,128)} %pressure.1, f32[64,64,128]{2,1,0:T(8,128)} %conduct.1, f32[64,64,128]{2,1,0:T(8,128)} %sat_new.1, f32[64,64,128]{2,1,0:T(8,128)} %sat_old.1, ...), custom_call_target="tpu_custom_call" | custom-call | tf_op jit(solution)/shard_map/local/pallas_call | solution.py:400
  13.7 0.0 copy-done
  13.7 0.0 copy-done.1
  13.8 0.0 copy-done.2
  13.8 29.0 %shared.1 = (f32[4,64,512]{2,1,0:T(8,128)S(1)}, f32[4,64,128]{2,1,0:T(8,128)S(1)}, f32[1,1]{1,0:T(1,128)}) custom-call(f32[1024,128]{1,0:T(8,128)S(1)} %get-tuple-element.10.partial, f32[4,64,128]{2,1,0:T(8,128)S(1)} %get-tuple-element.11.balance_in, f32[2,3,64,128]{3,2,1,0:T(8,128)S(1)} %get-tuple-element.12.edges, f32[8,128]{1,0:T(8,128)S(1)} %get-tuple-element.13.peak_in, ...), custom_call_target="tpu_custom_call" | custom-call | tf_op jit(solution)/shard_map/shared/pallas_call | solution.py:436
  42.8 0.8 %copy.16 = f32[4,64,512]{2,1,0:T(8,128)} copy(f32[4,64,512]{2,1,0:T(8,128)S(1)} %get-tuple-element.20) | data formatting | bytes 1048576
  43.6 0.7 %copy.17 = f32[4,64,128]{2,1,0:T(8,128)} copy(f32[4,64,128]{2,1,0:T(8,128)S(1)} %get-tuple-element.21) | data formatting | bytes 262144
Async XLA Ops:
  0.6 13.1 %copy-start = (s32[64,128]{1,0:T(8,128)S(1)}, s32[64,128]{1,0:T(8,128)}, u32[]{:S(2)}) copy-start(s32[64,128]{1,0:T(8,128)} %labels.3) | copy-start | bytes 98308
  0.6 13.1 %copy-start.1 = (s32[64,128]{1,0:T(8,128)S(1)}, s32[64,128]{1,0:T(8,128)}, u32[]{:S(2)}) copy-start(s32[64,128]{1,0:T(8,128)} %outlet.3) | copy-start | bytes 98308
  0.7 13.1 %copy-start.2 = (f32[64]{0:T(128)S(1)}, f32[64]{0:T(128)}, u32[]{:S(2)}) copy-start(f32[64]{0:T(128)} %param.17) | copy-start | bytes 772
